TPU v7x, 16 devices: a 4x2x1 block of a 4x4x8 slice. The times are simulated.
16 devices in a mesh: data: 2 (over y, z), cp: 8 (over x, core).
Axes of the slice: x: 4, y: 2, z: 1, core: 2. Of those that a mesh axis runs over, the one named last changes fastest.
The devices are a block of a 4x4x8 slice.
Arguments:
- x_tokens: bfloat16 [32, 2048, 4096], P('data', 'cp'), parts along dimension 0
- positions: int32 [32, 2048], P('data', 'cp'), parts along dimension 0
- w_query: bfloat16 [4096, 4096], replicated
- w_key: bfloat16 [4096, 1024], replicated
- w_value: bfloat16 [4096, 1024], replicated
- w_out: bfloat16 [4096, 4096], replicated
Outputs:
- output: bfloat16 [32, 2048, 4096], P('data', 'cp'), parts along dimension 0
There are 2 independent parts. A program takes and returns all parts, laid end to end along the dimension named above; an argument that names none is the same for every part.
All inputs are finite; a program needn't handle non-finite values.
Results may differ from a plain program's by a relative error of at most 0.0046917.
Values are sent between devices in bfloat16 or wider.
A program may use at most 768 MiB of HBM per device.

v0:
```python
import functools
import math

import jax
import jax.numpy as jnp
from jax import lax
from jax.experimental import pallas as pl
from jax.experimental.pallas import tpu as pltpu
from jax.sharding import PartitionSpec as P

HEAD_DIM = 128
ROPE_BASE = 500000
MASK_FILL = -1e30
EXP_SCALE = float(HEAD_DIM ** -0.5 * math.log2(math.e))
CORES = 2
ROWS = 2
TILE = 1024
GROUP = 4
PAIR = 256
VMEM_LIMIT = 66_000_000
LAG = 3
DELAY = 3
BACK = (6, 9)
EPI = 3
AHEAD = 6
SINGLE = 3
SPREAD = 3
COST = (4.7, 4.65, 1.6, 22.8, 1.75, 18.0)
SPLIT = 4
R1, L1, X0, R2, L2, X1, X2, X3 = range(8)
f32, bf16 = jnp.float32, jnp.bfloat16
div, rem = lax.div, lax.rem


def rope_tables(positions):
    half = HEAD_DIM // 2
    inv_freq = 1.0 / (ROPE_BASE ** (jnp.arange(0, HEAD_DIM, 2, dtype=f32) / HEAD_DIM))
    half_len = positions.shape[1] // 2
    pos = positions.astype(f32)
    front = jnp.broadcast_to(pos[:, :half_len, None], pos[:, :half_len].shape + (half,))
    back = jnp.broadcast_to(pos[:, half_len:, None], front.shape)
    angles = (jnp.concatenate([front, back], axis=-1) * jnp.concatenate([inv_freq, inv_freq])).reshape(-1, HEAD_DIM)
    return jnp.cos(angles), jnp.sin(angles)


def attn_scratch(cp, half_len):
    steps, fixed = cp + 1, cp // 2
    keys = 2 * half_len
    groups = lambda *shape: [pltpu.VMEM(shape, f32), pltpu.VMEM(shape, f32)]
    return [
        pltpu.VMEM((2, cp, 2, 2, GROUP, HEAD_DIM, half_len), bf16),
        *groups(steps, keys, PAIR),
        *groups(1 + len(BACK), HEAD_DIM, PAIR),
        *groups(fixed, HEAD_DIM, PAIR),
        *groups(2, 1, PAIR),
        *groups(2, 1, PAIR),
        pltpu.VMEM((2, keys, half_len), f32),
    ]


def attn_init(cp, scratch):
    _, _, _, _, _, pv0, pv1, _, _, _, _, bias = scratch
    keys, half_len = bias.shape[1:]
    kpos = lax.broadcasted_iota(jnp.int32, (keys, half_len), 0)
    qpos = lax.broadcasted_iota(jnp.int32, (keys, half_len), 1)
    for ref in (pv0, pv1):
        ref[ref.shape[0] - 1] = jnp.zeros(ref.shape[1:], f32)
    for p in range(2):
        bias[p] = jnp.where(kpos - qpos <= p * half_len, 0.0, MASK_FILL)


def attn_step(n, cp, my, q_ref, put, scratch):
    kvbuf, sc0, sc1, ac0, ac1, pv0, pv1, mx0, mx1, sm0, sm1, bias = scratch
    sbuf, acc, pvb, mst, lst = (sc0, sc1), (ac0, ac1), (pv0, pv1), (mx0, mx1), (sm0, sm1)
    steps, fixed = cp + 1, cp // 2
    half_len = kvbuf.shape[6]
    here = (rem(div(n, GROUP), 2), rem(n, GROUP))
    before = jnp.maximum(n - 1, 0)
    behind_ = (rem(div(before, GROUP), 2), rem(before, GROUP))
    nf, par = div(my, 2) + 1, rem(my, 2)

    def plan(t):
        if t == 0:
            return 0, nf - 1
        if t >= fixed:
            return 1, t - nf
        front = t < nf
        return jnp.where(front, 0, 1), jnp.where(front, t - 1, t - nf)

    def places(u):
        out = []
        for j in (2 * u, 2 * u + 1):
            front = j < cp
            out.append((jnp.where(front, j, 2 * cp - 1 - j), jnp.where(front, 0, 1)))
        return out

    plans = [plan(t) for t in range(steps)]
    locs = [places(u) for _, u in plans]
    low = jnp.full((1, PAIR), MASK_FILL, f32)
    zero = jnp.zeros((1, PAIR), f32)

    def scores(t, g):
        slot, e = here
        k = jnp.concatenate([kvbuf[slot, s, 0, f, e] for s, f in locs[t]], axis=0)
        s = lax.dot_general(k, q_ref[plans[t][0], 2 * g:2 * g + 2].reshape(PAIR, HEAD_DIM), (((1,), (1,)), ((), ())), preferred_element_type=f32)
        if t == 0 or t == steps - 1:
            b = bias[par if t == 0 else 1 - par]
            s = s + jnp.concatenate([b, b], axis=1)
        sbuf[g][t] = s
        return jnp.max(s, axis=0, keepdims=True)

    def finish_max(g, ms):
        front_max, back_max = ms[0], functools.reduce(jnp.maximum, ms[fixed:])
        for t in range(1, fixed):
            front = t < nf
            front_max = jnp.maximum(front_max, jnp.where(front, ms[t], low))
            back_max = jnp.maximum(back_max, jnp.where(front, low, ms[t]))
        mst[g][0] = front_max
        mst[g][1] = back_max

    def soft(t, g, behind):
        m = mst[g][plans[t][0]]
        if behind is not None:
            m = jnp.maximum(m, jnp.minimum(behind, MASK_FILL))
        p = jnp.exp2((sbuf[g][t] - m) * EXP_SCALE)
        return jnp.sum(p, axis=0, keepdims=True), p.astype(bf16)

    def weighted(ts, ps, at):
        slot, e = at
        vals = jnp.concatenate([kvbuf[slot, s, 1, f, e] for t in ts for s, f in locs[t]], axis=1)
        p = ps[0] if len(ps) == 1 else jnp.concatenate(ps, axis=0)
        return lax.dot_general(vals, p, (((1,), (0,)), ((), ())), preferred_element_type=f32)

    def epilogue(g):
        for half in range(2):
            inv = 1.0 / lst[g][half]
            for e in range(PAIR // HEAD_DIM):
                lanes = slice(e * half_len, (e + 1) * half_len)
                o = acc[g][half, :, lanes]
                for i in range(1, len(BACK) if half else 1):
                    o = o + acc[g][1 + i, :, lanes]
                for t in range(1, fixed):
                    mine = t < nf if half == 0 else t >= nf
                    o = o + pvb[g][jnp.where(mine, t - 1, fixed - 1), :, lanes]
                put(half, g * (PAIR // HEAD_DIM) + e, (o * inv[:, lanes]).astype(bf16).T)
                yield

    def put_weighted(g, ts, ps, at):
        out = weighted(ts, ps, at)
        if ts[0] == 0:
            acc[g][0] = out
        elif ts[0] < fixed:
            pvb[g][ts[0] - 1] = out
        else:
            acc[g][1 + BACK.index(ts[-1] + 1)] = out

    pending = []

    def drain(limit):
        while len(pending) > limit:
            put_weighted(*pending.pop(0))

    for g1, g2, at in ((0, 1, behind_), (1, 0, here)):
        epi = epilogue(g1)
        ms, lf, lb, held = [], None, zero, []
        for t in range(steps):
            ms.append(scores(t, g1))
            l, p = soft(t, g2, ms[t - LAG] if t >= LAG else None)
            if t < fixed:
                front = t < nf
                lf = l if t == 0 else lf + jnp.where(front, l, zero)
                lb = lb if t == 0 else lb + jnp.where(front, zero, l)
                pending.append((g2, [t], [p], at))
            else:
                lb = lb + l
                held.append(p)
                if t + 1 in BACK:
                    pending.append((g2, list(range(t + 1 - len(held), t + 1)), held, at))
                    held = []
            drain(DELAY)
            if t >= EPI:
                next(epi, None)
        lst[g2][0] = lf
        lst[g2][1] = lb
        finish_max(g1, ms)
        for _ in epi:
            pass
    drain(0)


def plan_steps(chunks, n_proj, n_out, per_chunk, send_at):
    seq = [('P', i) for i in range(AHEAD * n_proj)]
    p, o = AHEAD * n_proj, 0
    for c in range(chunks):
        seq += [('A', c * per_chunk + i) for i in range(per_chunk)]
        if c >= chunks - SINGLE:
            seq.append(('S', (c + 1) * per_chunk))
        end = n_out * (c + 1 if c >= chunks - SINGLE else c)
        seq += [('O', i) for i in range(o, end)]
        o = end
        if p < chunks * n_proj:
            seq += [('P', p + i) for i in range(SPREAD)]
            p += SPREAD
            if p == chunks * n_proj:
                seq.append(('F', 0))
    units = [(c * ROWS, ROWS) for c in range(chunks - SINGLE)] + [(i, 1) for i in range((chunks - SINGLE) * ROWS, chunks * ROWS)]
    first_use = [seq.index(('A', row * per_chunk // ROWS)) for row, _ in units]
    proj, out, att, wire, inner, now = COST
    took = {'P': proj, 'O': out, 'A': att, 'S': att, 'F': 0.6}
    hops = {'own': [], 'one': [], 'two': [], 'three': [], 'in': []}
    link, core, got1, got2, sent = 0.0, 0.0, {}, {}, -1
    for step, (kind, i) in enumerate(seq):
        if step and seq[step - 1][0] == 'P' and seq[step - 1][1] % n_proj == send_at:
            sent = seq[step - 1][1] // n_proj
            hops['own'].append(step)
        must = max((u for u in range(len(units)) if first_use[u] <= step + 1), default=-1)
        done = lambda name: len(hops[name])
        while done('one') < len(units) or done('two') < len(units):
            u = done('two')
            if done('one') < min(u + 2, len(units)):
                u = done('one')
                if units[u][0] // ROWS > sent:
                    break
                link = max(now, link) + wire * units[u][1]
                got1[u] = link
                hops['one'].append(step)
            else:
                if now < got1[u] + 3 and u > must:
                    break
                now = max(now, got1[u])
                link = max(now, link) + wire * units[u][1] / 2
                core = max(now, core) + 2 * inner * units[u][1]
                got2[u] = max(link, core)
                hops['two'].append(step)
        while done('three') < done('two') and (got2[done('three')] + 3 <= now or done('three') <= must):
            u = done('three')
            now = max(now, got2[u])
            core = max(now, core) + inner * units[u][1]
            hops['three'].append(step)
        now += took[kind]
    for u in range(len(units)):
        hops['in'].append(first_use[u] - 1)
    return seq, units, hops


def layer(mesh, x_loc, cosine, sine, w_query, w_key, w_value, w_out):
    cp = mesh.shape['cp']
    rows, tok_rows, depth = x_loc.shape
    half_len = tok_rows // 2
    inner, kv_cols = w_query.shape[1], w_key.shape[1]
    heads = kv_cols // HEAD_DIM
    group_cols = inner // heads
    per_tile, fold = TILE // HEAD_DIM, TILE // HEAD_DIM // GROUP
    toks = ROWS * tok_rows
    chunks = rows // ROWS
    kt, qt, n_out = kv_cols // TILE, inner // TILE, depth // TILE
    n_proj = 2 * kt + qt
    per_chunk = ROWS * heads
    total = rows * heads
    n_groups = heads // GROUP
    assert n_groups == 2
    assert depth == w_query.shape[0] and group_cols == 2 * PAIR and n_proj % SPREAD == 0 and rows % ROWS == 0
    assert kt == 1 and SPREAD > 2 * kt and group_cols == GROUP * HEAD_DIM and cp // CORES == 4
    seq, units, hops = plan_steps(chunks, n_proj, n_out, per_chunk, 2 * kt)
    n_steps = len(seq)
    loops = (chunks - AHEAD) * n_proj // SPREAD
    assert 2 <= loops <= chunks - SINGLE
    first_a = seq.index(('A', 0))
    second_a = seq.index(('A', per_chunk))
    flush = seq.index(('F', 0))
    period = per_chunk + n_out + SPREAD
    ends = [i for i in range(flush, n_steps) if i == flush or seq[i][0] != seq[i - 1][0]] + [n_steps]
    tail = [(start, seq[start]) for start in ends[:-1]]
    base = n_proj * AHEAD + SPREAD
    both = n_out + SPREAD
    last_both = base + both * (loops - 1)
    n_tiles = (n_proj + n_out) * chunks

    def pick(cases, other):
        for cond, val in reversed(cases):
            other = jnp.where(cond, val, other)
        return other

    def kern(x_hbm, cos_ref, sin_ref, wq_hbm, wk_hbm, wv_hbm, wo_hbm, y_hbm, kv_hbm, q_hbm,
             wbuf, xbuf, xres, raw, stage, oscr, ybuf, qbuf,
             wsem, xsem, rsem, osem, ysem, qsem, kvsem, send_sem, recv_sem, *attn):
        s = pl.program_id(0)
        my = lax.axis_index('cp')
        chip, core = div(my, CORES), rem(my, CORES)
        chips = cp // CORES

        def device(chip_shift, core_shift=0):
            return rem(chip + chip_shift, chips) * CORES + rem(core + core_shift, CORES)

        nxt, far, prv, mate = device(1), device(2), device(chips - 1), device(0, 1)

        a, r = 1 + div(s - second_a, period), rem(s - second_a, period)
        r0 = s - first_a
        kinds = {'A': 0, 'S': 1, 'O': 2, 'P': 3, 'F': 4}
        parts = [
            (s < first_a, 3, s),
            (s < first_a + per_chunk, 0, r0),
            (s < second_a, 3, s - per_chunk),
            (s < flush, jnp.where(r < per_chunk, 0, jnp.where(r < per_chunk + n_out, 2, 3)),
             jnp.where(r < per_chunk, a * per_chunk + r,
                       jnp.where(r < per_chunk + n_out, (a - 1) * n_out + r - per_chunk, AHEAD * n_proj + a * SPREAD + r - per_chunk - n_out))),
        ]
        for (start, (what, i)), (stop, _) in zip(tail, tail[1:] + [(n_steps, None)]):
            parts.append((s < stop, kinds[what], s + (i - start)))
        kind = pick([(c, k) for c, k, _ in parts[:-1]], parts[-1][1])
        num = pick([(c, i) for c, _, i in parts[:-1]], parts[-1][2])
        is_new, is_skew, is_out, is_proj, is_flush = (kind == k for k in range(5))
        is_head = kind < 2
        n = oidx = pidx = num
        oc, col = div(oidx, n_out), rem(oidx, n_out)
        pc, pt = div(pidx, n_proj), rem(pidx, n_proj)
        tile_p = jnp.where(pidx < base, pidx, base + div(pidx - base, SPREAD) * both + n_out + rem(pidx - base, SPREAD))
        tile_o = jnp.where(oc < loops - 1, base + oc * both + col, last_both + oidx - (loops - 1) * n_out)

        def row_ds(c):
            return pl.ds(c * ROWS, ROWS)

        def load_tile(j):
            slot = rem(j, 2)
            u = j - base
            v = j - last_both
            only_out = j >= last_both
            is_p = jnp.logical_or(j < base, jnp.logical_and(jnp.logical_not(only_out), rem(u, both) >= n_out))
            p = rem(jnp.where(j < base, j, base + div(u, both) * SPREAD + rem(u, both) - n_out), n_proj)
            o_col = jnp.where(only_out, rem(v, n_out), rem(u, both))
            o_chunk = jnp.where(only_out, loops - 1 + div(v, n_out), div(u, both))

            def start(w_hbm, tile_col):
                cols = pl.ds(pl.multiple_of(tile_col * TILE, TILE), TILE)
                part = w_hbm.shape[0] // SPLIT
                for i in range(SPLIT):
                    ks = pl.ds(i * part, part)
                    pltpu.make_async_copy(w_hbm.at[ks, cols], wbuf.at[slot, ks], wsem.at[slot]).start()

            @pl.when(jnp.logical_and(is_p, p < kt))
            def _():
                start(wk_hbm, p)

            @pl.when(jnp.logical_and(is_p, jnp.logical_and(p >= kt, p < 2 * kt)))
            def _():
                start(wv_hbm, p - kt)

            @pl.when(jnp.logical_and(is_p, p >= 2 * kt))
            def _():
                start(wq_hbm, p - 2 * kt)

            @pl.when(jnp.logical_not(is_p))
            def _():
                start(wo_hbm, o_col)
                load_res(o_chunk, o_col, slot).start()

        def load_res(c, tile_col, slot):
            cols = pl.ds(pl.multiple_of(tile_col * TILE, TILE), TILE)
            return pltpu.make_async_copy(x_hbm.at[row_ds(c), :, cols], xres.at[slot], rsem.at[slot])

        def next_tile(j):
            @pl.when(j + 1 < n_tiles)
            def _():
                load_tile(j + 1)
            slot = rem(j, 2)
            pltpu.make_async_copy(wo_hbm.at[:, pl.ds(0, TILE)], wbuf.at[slot], wsem.at[slot]).wait()
            return slot

        def load_x(c):
            return pltpu.make_async_copy(x_hbm.at[row_ds(c)], xbuf.at[rem(c, 2)], xsem.at[rem(c, 2)])

        def load_q(m):
            return pltpu.make_async_copy(q_hbm.at[div(m, heads), rem(m, heads)], qbuf.at[rem(m, 2)], qsem.at[rem(m, 2)])

        def load_kv(g):
            slot = rem(g, 2)
            return [pltpu.make_async_copy(kv_hbm.at[div(g, n_groups), src, rem(g, n_groups)], attn[0].at[slot, src], kvsem.at[slot]) for src in range(cp)]

        def wait_kv(g):
            slot = rem(g, 2)
            pltpu.make_async_copy(kv_hbm.at[0, :, 0], attn[0].at[slot], kvsem.at[slot]).wait()

        def store_y(c, tile_col, slot):
            cols = pl.ds(pl.multiple_of(tile_col * TILE, TILE), TILE)
            return pltpu.make_async_copy(ybuf.at[slot], y_hbm.at[row_ds(c), :, cols], ysem.at[slot])

        def hop(kind, row, size, part=None):
            rs = pl.ds(row, size)
            src, to = {R1: (my, nxt), L1: (my, prv), X0: (my, mate), R2: (prv, nxt), L2: (nxt, prv), X1: (nxt, mate), X2: (far, mate), X3: (prv, mate)}[kind]
            ref = kv_hbm.at[rs, src]
            if kind in (R2, L2):
                group = 0 if kind == R2 else 1
                ref = kv_hbm.at[rs, src, group] if part is None else kv_hbm.at[rs, src, group, part]
            elif part is not None:
                ref = kv_hbm.at[rs, src, part]
            sem = 2 * row + (part or 0)
            return pltpu.make_async_remote_copy(src_ref=ref, dst_ref=ref, send_sem=send_sem.at[kind, sem], recv_sem=recv_sem.at[kind, sem],
                                                device_id={'cp': to}, device_id_type=pl.DeviceIdType.MESH)

        def ring(kinds, row, size, act):
            @pl.when(core == 0)
            def _():
                near(kinds, row, size, act)

            @pl.when(jnp.logical_and(core != 0, size == 1))
            def _():
                for kind in kinds:
                    for part in range(2):
                        act(hop(kind, row, 1, part))

            @pl.when(jnp.logical_and(core != 0, size != 1))
            def _():
                for kind in kinds:
                    for i in range(ROWS):
                        act(hop(kind, row + i, 1))

        def near(kinds, row, size, act):
            @pl.when(size == 1)
            def _():
                for kind in kinds:
                    act(hop(kind, row, 1))

            @pl.when(size != 1)
            def _():
                for kind in kinds:
                    act(hop(kind, row, ROWS))

        start, received, left = (lambda c: c.start()), (lambda c: c.wait_recv()), (lambda c: c.wait_send())

        def hop_one(row, size):
            ring((R1, L1), row, size, start)
            near((X0,), row, size, start)

        def hop_two(row, size):
            ring((R1, L1), row, size, received)
            ring((R2, L2), row, size, start)
            near((X1, X3), row, size, start)

        def hop_three(row, size):
            ring((R2, L2), row, size, received)
            near((X2,), row, size, start)

        def arrive(row, size):
            near((X0, X1, X3, X2), row, size, received)
            ring((R1, L1, R2, L2), row, size, left)
            near((X0, X1, X3, X2), row, size, left)
            for copy in load_kv(row * n_groups):
                copy.start()

            @pl.when(row == 0)
            def _():
                load_q(0).start()

        def own_stored(row, size):
            first = div(row, ROWS) * n_proj
            wait_store(first)
            wait_store(first + 1)

        def unit_hops(lo, hi):
            for name, act in (('own', own_stored), ('two', hop_two), ('one', hop_one), ('three', hop_three), ('in', arrive)):
                due = [(step, (u * ROWS, ROWS) if name == 'own' else units[u]) for u, step in enumerate(hops[name]) if lo <= step < hi]
                if not due:
                    continue
                row, size = pick([(s == step, row) for step, (row, _) in due], -1), pick([(s == step, size) for step, (_, size) in due], ROWS)

                @pl.when(row >= 0)
                def _(row=row, size=size, act=act):
                    act(row, size)

        @pl.when(s == 0)
        def _():
            barrier = pltpu.get_barrier_semaphore()
            for to in (nxt, prv, mate):
                pl.semaphore_signal(barrier, inc=1, device_id={'cp': to}, device_id_type=pl.DeviceIdType.MESH)
            load_x(0).start()
            load_tile(0)
            attn_init(cp, attn)
            pl.semaphore_wait(barrier, 3)

        def store_tile(p):
            c, tile, slot = div(p, n_proj), rem(p, n_proj), rem(p, 2)
            rs = row_ds(c)

            @pl.when(tile < 2)
            def _():
                pltpu.make_async_copy(stage.at[slot], kv_hbm.at[rs, my, :, tile], osem.at[slot]).start()

            @pl.when(tile >= 2)
            def _():
                pltpu.make_async_copy(stage.at[slot], q_hbm.at[rs, pl.ds((tile - 2) * fold, fold)], osem.at[slot]).start()

        def wait_store(p):
            slot = rem(p, 2)
            pltpu.make_async_copy(stage.at[slot], q_hbm.at[pl.ds(0, ROWS), pl.ds(0, fold)], osem.at[slot]).wait()

        def rope_epilogue(p):
            c, slot = div(p, n_proj), rem(p, 2)
            is_v = rem(p, n_proj) == 1
            low_lanes = lax.broadcasted_iota(jnp.int32, (half_len, HEAD_DIM), 1) < HEAD_DIM // 2
            for i in range(ROWS):
                ts = pl.ds(pl.multiple_of((c * ROWS + i) * half_len, half_len), half_len)
                cos, sin = cos_ref[ts], sin_ref[ts]
                cos_r, sin_r = pltpu.roll(cos, HEAD_DIM // 2, 1), pltpu.roll(sin, HEAD_DIM // 2, 1)
                for half in range(2):
                    cos_h = jnp.where(low_lanes, cos, cos_r) if half == 0 else jnp.where(low_lanes, cos_r, cos)
                    sin_h = jnp.where(low_lanes, -sin, sin_r) if half == 0 else jnp.where(low_lanes, -sin_r, sin)
                    rs = slice(i * tok_rows + half * half_len, i * tok_rows + (half + 1) * half_len)
                    for e in range(per_tile):
                        vals = raw[rs, e * HEAD_DIM:(e + 1) * HEAD_DIM]
                        wide = vals.astype(f32)
                        turned = (wide * cos_h + pltpu.roll(wide, HEAD_DIM // 2, 1) * sin_h).astype(bf16)
                        stage[slot, i, e // GROUP, half, e % GROUP] = jnp.where(is_v, vals.T, turned)

        @pl.when(is_proj)
        def _():
            next_tile(tile_p)

            @pl.when(jnp.logical_and(pidx >= 3, jnp.logical_or(pt < 3, pt > 4)))
            def _():
                wait_store(pidx - 3)

            @pl.when(pt == 0)
            def _():
                load_x(pc).wait()

            @pl.when(jnp.logical_and(pt == 1, pc + 1 < chunks))
            def _():
                load_x(pc + 1).start()

        spans = 4
        for i in range(spans):
            lo, hi = n_steps * i // spans, n_steps * (i + 1) // spans

            @pl.when(jnp.logical_and(s >= lo, s < hi))
            def _(lo=lo, hi=hi):
                unit_hops(lo, hi)

        @pl.when(is_proj)
        def _():
            rope_epilogue(jnp.maximum(pidx - 1, 0))
            x = xbuf[rem(pc, 2)].reshape(toks, depth)
            raw[...] = jnp.dot(x, wbuf[rem(tile_p, 2)], preferred_element_type=f32).astype(bf16)

            @pl.when(pidx >= 1)
            def _():
                store_tile(pidx - 1)

        @pl.when(is_flush)
        def _():
            end = n_proj * chunks
            wait_store(end - 3)
            rope_epilogue(end - 1)
            store_tile(end - 1)
            wait_store(end - 2)
            wait_store(end - 1)

        @pl.when(is_head)
        def _():
            g = div(n, GROUP)

            @pl.when(jnp.logical_and(n < total, jnp.logical_or(is_skew, jnp.logical_or(rem(n, per_chunk) != 0, n <= total - SINGLE * per_chunk))))
            def _():
                load_q(n).wait()

            @pl.when(is_new)
            def _():
                @pl.when(n + 1 < total)
                def _():
                    load_q(n + 1).start()

                @pl.when(rem(n, GROUP) == 0)
                def _():
                    wait_kv(g)

                fresh = jnp.logical_or(rem(g + 1, ROWS * n_groups) == 0, jnp.logical_and(g + 1 >= (rows - SINGLE * ROWS) * n_groups, rem(g + 1, n_groups) == 0))

                @pl.when(jnp.logical_and(rem(n, GROUP) == 1, jnp.logical_not(fresh)))
                def _():
                    for copy in load_kv(g + 1):
                        copy.start()

            m = jnp.maximum(n - 1, 0)
            o_slot = rem(div(m, per_chunk), 2)
            row, head = rem(div(m, heads), ROWS), rem(m, heads)

            def put(half, j, val):
                rs = pl.ds(pl.multiple_of(row * tok_rows + half * half_len, half_len), half_len)
                cs = pl.ds(pl.multiple_of(head * group_cols + j * HEAD_DIM, HEAD_DIM), HEAD_DIM)
                oscr[o_slot, rs, cs] = val

            attn_step(n, cp, my, qbuf.at[rem(n, 2)], put, attn)

        @pl.when(is_out)
        def _():
            slot = next_tile(tile_o)
            y_slot = rem(oidx, 2)
            load_res(oc, col, slot).wait()

            @pl.when(oidx >= 2)
            def _():
                store_y(0, 0, y_slot).wait()

            out = jnp.dot(oscr[rem(oc, 2)], wbuf[slot], preferred_element_type=f32)
            ybuf[y_slot] = (xres[slot].astype(f32) + out.reshape(ROWS, tok_rows, TILE)).astype(bf16)
            store_y(oc, col, y_slot).start()

            @pl.when(oidx == n_out * chunks - 1)
            def _():
                store_y(0, 0, 1 - y_slot).wait()
                store_y(0, 0, y_slot).wait()

    any_spec = pl.BlockSpec(memory_space=pl.ANY)
    flops = 2 * rows * tok_rows * depth * (2 * inner + 2 * kv_cols) + 8 * total * (cp + 1) * half_len * group_cols * HEAD_DIM * 2
    y, _, _ = pl.pallas_call(
        kern,
        name='layer',
        grid=(n_steps,),
        in_specs=[any_spec, pl.BlockSpec(memory_space=pltpu.VMEM), pl.BlockSpec(memory_space=pltpu.VMEM)] + [any_spec] * 4,
        out_specs=[any_spec] * 3,
        out_shape=[
            jax.ShapeDtypeStruct(x_loc.shape, bf16),
            jax.ShapeDtypeStruct((rows, cp, n_groups, 2, 2, GROUP, half_len, HEAD_DIM), bf16),
            jax.ShapeDtypeStruct((rows, heads, 2, group_cols // HEAD_DIM, half_len, HEAD_DIM), bf16),
        ],
        scratch_shapes=[
            pltpu.VMEM((2, depth, TILE), bf16),
            pltpu.VMEM((2, ROWS, tok_rows, depth), bf16),
            pltpu.VMEM((2, ROWS, tok_rows, TILE), bf16),
            pltpu.VMEM((toks, TILE), bf16),
            pltpu.VMEM((2, ROWS, fold, 2, GROUP, half_len, HEAD_DIM), bf16),
            pltpu.VMEM((2, toks, inner), bf16),
            pltpu.VMEM((2, ROWS, tok_rows, TILE), bf16),
            pltpu.VMEM((2, 2, group_cols // HEAD_DIM, half_len, HEAD_DIM), bf16),
            pltpu.SemaphoreType.DMA((2,)),
            pltpu.SemaphoreType.DMA((2,)),
            pltpu.SemaphoreType.DMA((2,)),
            pltpu.SemaphoreType.DMA((2,)),
            pltpu.SemaphoreType.DMA((2,)),
            pltpu.SemaphoreType.DMA((2,)),
            pltpu.SemaphoreType.DMA((2,)),
            pltpu.SemaphoreType.DMA((8, 2 * rows)),
            pltpu.SemaphoreType.DMA((8, 2 * rows)),
        ] + attn_scratch(cp, half_len),
        compiler_params=pltpu.CompilerParams(dimension_semantics=('arbitrary',), collective_id=0, has_side_effects=True, vmem_limit_bytes=VMEM_LIMIT),
        cost_estimate=pl.CostEstimate(flops=flops, bytes_accessed=4 * rows * tok_rows * depth, transcendentals=0),
    )(x_loc, cosine, sine, w_query, w_key, w_value, w_out)
    return y


def solution(mesh):
    row_spec, pos_spec, rep_spec = P('data', 'cp', None), P('data', 'cp'), P(None, None)

    def local_block(x_loc, pos_loc, w_query, w_key, w_value, w_out):
        cosine, sine = rope_tables(pos_loc)
        return layer(mesh, x_loc, cosine, sine, w_query, w_key, w_value, w_out)

    return jax.shard_map(local_block, mesh=mesh, in_specs=(row_spec, pos_spec, rep_spec, rep_spec, rep_spec, rep_spec), out_specs=row_spec, check_vma=False)
```

profile of v0, /device:TPU:113, one launch (start us, length us, event | category | flops | bytes accessed | tf_op | source)
XLA Modules:
  0.0 686.9 jit_solution(9163040586270268556)
XLA Ops:
  0.0 0.1 pad_maximum_fusion
  0.1 0.7 convert_element_type.3
  0.8 0.3 broadcast_in_dim.18
  1.2 0.3 broadcast_in_dim.20
  1.5 4.9 fusion
  6.4 657.6 %layer.1 = (bf16[16,256,4096]{2,1,0:T(8,128)(2,1)}, bf16[16,8,2,2,2,4,128,128]{7,6,5,4,3,2,1,0:T(8,128)(2,1)}, bf16[16,8,2,4,128,128]{5,4,3,2,1,0:T(8,128)(2,1)}) custom-call(bf16[16,256,4096]{2,1,0:T(8,128)(2,1)} %x_hbm.1, f32[2048,128]{1,0:T(8,128)} %get-tuple-element.8.cos_ref, f32[2048,128]{1,0:T(8,128)} %get-tuple-element.7.sin_ref, ...), custom_call_target="tpu_custom_call" | custom-call | flops 498216206336 | bytes 67108864 | tf_op jit(solution)/shard_map/layer/pallas_call | solution.py:614
  664.0 22.9 %copy.8 = bf16[16,256,4096]{2,1,0:T(8,128)(2,1)} copy(bf16[16,256,4096]{2,1,0:T(8,128)(2,1)} %get-tuple-element.6) | data formatting | bytes 67108864
  (2 shorter events, 0.0 us)
where the time goes:
time: 687 us
  Pallas kernels  658 us (96%)
  local copies, waits for them, and re-layouts  23.6 us (3%)
    pallas_call x1, Pallas kernels, layer(): pl.pallas_call(kern, name='layer', grid=(n_steps,), in_specs=[any_spec, p...  658 us
    unnamed x1, local copies, waits for them, and re-layouts  22.9 us

commit v1 on v0

--- a/solution.py
+++ b/solution.py
@@ -18,15 +18,13 @@
 GROUP = 4
 PAIR = 256
 VMEM_LIMIT = 66_000_000
-LAG = 3
-DELAY = 3
-BACK = (6, 9)
+LAG = 5
+DELAY = 2
+BACK = (2, 0)
 EPI = 3
-AHEAD = 6
-SINGLE = 3
-SPREAD = 3
-COST = (4.7, 4.65, 1.6, 22.8, 1.75, 18.0)
-SPLIT = 4
+SINGLE = 2
+COST = (4.85, 4.72, 1.6, 22.8, 0.3, 1.75, 18.0)
+SPLIT = 2
 R1, L1, X0, R2, L2, X1, X2, X3 = range(8)
 f32, bf16 = jnp.float32, jnp.bfloat16
 div, rem = lax.div, lax.rem
@@ -43,93 +41,117 @@
     return jnp.cos(angles), jnp.sin(angles)
 
 
+def attn_steps(cp):
+    dyn = cp // 2 - 1
+    return ['front'] + ['extra'] + [('pair', k) for k in range(dyn)] + ['back'] + [('pair', k) for k in range(dyn, cp - 1)]
+
+
 def attn_scratch(cp, half_len):
-    steps, fixed = cp + 1, cp // 2
-    keys = 2 * half_len
+    steps = attn_steps(cp)
+    blocks = sum(1 if isinstance(t, str) else 2 for t in steps)
     groups = lambda *shape: [pltpu.VMEM(shape, f32), pltpu.VMEM(shape, f32)]
     return [
         pltpu.VMEM((2, cp, 2, 2, GROUP, HEAD_DIM, half_len), bf16),
-        *groups(steps, keys, PAIR),
+        *groups(blocks * half_len, PAIR),
         *groups(1 + len(BACK), HEAD_DIM, PAIR),
-        *groups(fixed, HEAD_DIM, PAIR),
+        *groups(cp // 2 + 1, HEAD_DIM, PAIR),
         *groups(2, 1, PAIR),
         *groups(2, 1, PAIR),
-        pltpu.VMEM((2, keys, half_len), f32),
+        pltpu.VMEM((half_len, half_len), f32),
     ]
 
 
 def attn_init(cp, scratch):
     _, _, _, _, _, pv0, pv1, _, _, _, _, bias = scratch
-    keys, half_len = bias.shape[1:]
-    kpos = lax.broadcasted_iota(jnp.int32, (keys, half_len), 0)
-    qpos = lax.broadcasted_iota(jnp.int32, (keys, half_len), 1)
+    kpos = lax.broadcasted_iota(jnp.int32, bias.shape, 0)
+    qpos = lax.broadcasted_iota(jnp.int32, bias.shape, 1)
     for ref in (pv0, pv1):
         ref[ref.shape[0] - 1] = jnp.zeros(ref.shape[1:], f32)
-    for p in range(2):
-        bias[p] = jnp.where(kpos - qpos <= p * half_len, 0.0, MASK_FILL)
+    bias[...] = jnp.where(kpos <= qpos, 0.0, MASK_FILL)
 
 
 def attn_step(n, cp, my, q_ref, put, scratch):
     kvbuf, sc0, sc1, ac0, ac1, pv0, pv1, mx0, mx1, sm0, sm1, bias = scratch
     sbuf, acc, pvb, mst, lst = (sc0, sc1), (ac0, ac1), (pv0, pv1), (mx0, mx1), (sm0, sm1)
-    steps, fixed = cp + 1, cp // 2
+    steps, parts = attn_steps(cp), cp // 2
     half_len = kvbuf.shape[6]
     here = (rem(div(n, GROUP), 2), rem(n, GROUP))
     before = jnp.maximum(n - 1, 0)
     behind_ = (rem(div(before, GROUP), 2), rem(before, GROUP))
-    nf, par = div(my, 2) + 1, rem(my, 2)
-
-    def plan(t):
-        if t == 0:
-            return 0, nf - 1
-        if t >= fixed:
-            return 1, t - nf
-        front = t < nf
-        return jnp.where(front, 0, 1), jnp.where(front, t - 1, t - nf)
-
-    def places(u):
-        out = []
-        for j in (2 * u, 2 * u + 1):
-            front = j < cp
-            out.append((jnp.where(front, j, 2 * cp - 1 - j), jnp.where(front, 0, 1)))
-        return out
-
-    plans = [plan(t) for t in range(steps)]
-    locs = [places(u) for _, u in plans]
+    pairs, par = div(my, 2), rem(my, 2)
+
+    def place(j):
+        front = j < cp
+        return jnp.where(front, j, 2 * cp - 1 - j), jnp.where(front, 0, 1)
+
+    front_of, part_of, locs, rows_of, row = {}, {}, {}, {}, 0
+    for t in steps:
+        if t == 'front':
+            front_of[t], blocks = True, [my]
+        elif t == 'back':
+            front_of[t], blocks = False, [2 * cp - 1 - my]
+        elif t == 'extra':
+            front_of[t], part_of[t], blocks = par == 1, 0, [jnp.where(par == 1, my - 1, 2 * cp - 2 - my)]
+        else:
+            k = t[1]
+            if k < parts - 1:
+                front_of[t], part_of[t] = k < pairs, 1 + k
+                first = 2 * jnp.where(k < pairs, k, k - pairs)
+            else:
+                front_of[t], first = False, 2 * (k - pairs)
+            blocks = [first, first + 1]
+        locs[t] = [place(j) for j in blocks]
+        rows_of[t] = slice(row, row + len(blocks) * half_len)
+        row += len(blocks) * half_len
     low = jnp.full((1, PAIR), MASK_FILL, f32)
     zero = jnp.zeros((1, PAIR), f32)
 
+    def half_of(t):
+        return jnp.where(front_of[t], 0, 1) if t in part_of else 0 if front_of[t] else 1
+
+    def stack(items, axis):
+        return items[0] if len(items) == 1 else jnp.concatenate(items, axis=axis)
+
     def scores(t, g):
         slot, e = here
-        k = jnp.concatenate([kvbuf[slot, s, 0, f, e] for s, f in locs[t]], axis=0)
-        s = lax.dot_general(k, q_ref[plans[t][0], 2 * g:2 * g + 2].reshape(PAIR, HEAD_DIM), (((1,), (1,)), ((), ())), preferred_element_type=f32)
-        if t == 0 or t == steps - 1:
-            b = bias[par if t == 0 else 1 - par]
+        k = stack([kvbuf[slot, s, 0, f, e] for s, f in locs[t]], 0)
+        s = lax.dot_general(k, q_ref[half_of(t), 2 * g:2 * g + 2].reshape(PAIR, HEAD_DIM), (((1,), (1,)), ((), ())), preferred_element_type=f32)
+        if t in ('front', 'back'):
+            b = bias[...]
             s = s + jnp.concatenate([b, b], axis=1)
-        sbuf[g][t] = s
+        sbuf[g][rows_of[t]] = s
         return jnp.max(s, axis=0, keepdims=True)
 
     def finish_max(g, ms):
-        front_max, back_max = ms[0], functools.reduce(jnp.maximum, ms[fixed:])
-        for t in range(1, fixed):
-            front = t < nf
-            front_max = jnp.maximum(front_max, jnp.where(front, ms[t], low))
-            back_max = jnp.maximum(back_max, jnp.where(front, low, ms[t]))
+        front_max, back_max = low, low
+        for t, m in zip(steps, ms):
+            if t in part_of:
+                front_max = jnp.maximum(front_max, jnp.where(front_of[t], m, low))
+                back_max = jnp.maximum(back_max, jnp.where(front_of[t], low, m))
+            elif front_of[t]:
+                front_max = jnp.maximum(front_max, m)
+            else:
+                back_max = jnp.maximum(back_max, m)
         mst[g][0] = front_max
         mst[g][1] = back_max
 
     def soft(t, g, behind):
-        m = mst[g][plans[t][0]]
+        m = mst[g][half_of(t)]
         if behind is not None:
             m = jnp.maximum(m, jnp.minimum(behind, MASK_FILL))
-        p = jnp.exp2((sbuf[g][t] - m) * EXP_SCALE)
+        p = jnp.exp2((sbuf[g][rows_of[t]] - m) * EXP_SCALE)
         return jnp.sum(p, axis=0, keepdims=True), p.astype(bf16)
 
-    def weighted(ts, ps, at):
+    def put_weighted(g, ts, ps, at):
         slot, e = at
-        vals = jnp.concatenate([kvbuf[slot, s, 1, f, e] for t in ts for s, f in locs[t]], axis=1)
-        p = ps[0] if len(ps) == 1 else jnp.concatenate(ps, axis=0)
-        return lax.dot_general(vals, p, (((1,), (0,)), ((), ())), preferred_element_type=f32)
+        vals = stack([kvbuf[slot, s, 1, f, e] for t in ts for s, f in locs[t]], 1)
+        out = lax.dot_general(vals, stack(ps, 0), (((1,), (0,)), ((), ())), preferred_element_type=f32)
+        if ts[0] in part_of:
+            pvb[g][part_of[ts[0]]] = out
+        elif front_of[ts[0]]:
+            acc[g][0] = out
+        else:
+            acc[g][1 + BACK.index(len(steps) - 1 - steps.index(ts[-1]))] = out
 
     def epilogue(g):
         for half in range(2):
@@ -139,20 +161,11 @@
                 o = acc[g][half, :, lanes]
                 for i in range(1, len(BACK) if half else 1):
                     o = o + acc[g][1 + i, :, lanes]
-                for t in range(1, fixed):
-                    mine = t < nf if half == 0 else t >= nf
-                    o = o + pvb[g][jnp.where(mine, t - 1, fixed - 1), :, lanes]
+                for t, part in part_of.items():
+                    mine = front_of[t] if half == 0 else jnp.logical_not(front_of[t])
+                    o = o + pvb[g][jnp.where(mine, part, parts), :, lanes]
                 put(half, g * (PAIR // HEAD_DIM) + e, (o * inv[:, lanes]).astype(bf16).T)
                 yield
-
-    def put_weighted(g, ts, ps, at):
-        out = weighted(ts, ps, at)
-        if ts[0] == 0:
-            acc[g][0] = out
-        elif ts[0] < fixed:
-            pvb[g][ts[0] - 1] = out
-        else:
-            acc[g][1 + BACK.index(ts[-1] + 1)] = out
 
     pending = []
 
@@ -162,26 +175,29 @@
 
     for g1, g2, at in ((0, 1, behind_), (1, 0, here)):
         epi = epilogue(g1)
-        ms, lf, lb, held = [], None, zero, []
-        for t in range(steps):
+        ms, front_sum, back_sum, held = [], zero, zero, []
+        for i, t in enumerate(steps):
             ms.append(scores(t, g1))
-            l, p = soft(t, g2, ms[t - LAG] if t >= LAG else None)
-            if t < fixed:
-                front = t < nf
-                lf = l if t == 0 else lf + jnp.where(front, l, zero)
-                lb = lb if t == 0 else lb + jnp.where(front, zero, l)
+            l, p = soft(t, g2, ms[i - LAG] if i >= LAG else None)
+            if t in part_of:
+                front_sum = front_sum + jnp.where(front_of[t], l, zero)
+                back_sum = back_sum + jnp.where(front_of[t], zero, l)
+            elif front_of[t]:
+                front_sum = front_sum + l
+            else:
+                back_sum = back_sum + l
+            if t in part_of or front_of[t]:
                 pending.append((g2, [t], [p], at))
             else:
-                lb = lb + l
-                held.append(p)
-                if t + 1 in BACK:
-                    pending.append((g2, list(range(t + 1 - len(held), t + 1)), held, at))
+                held.append((t, p))
+                if len(steps) - 1 - i in BACK:
+                    pending.append((g2, [t for t, _ in held], [p for _, p in held], at))
                     held = []
             drain(DELAY)
-            if t >= EPI:
+            if i >= EPI:
                 next(epi, None)
-        lst[g2][0] = lf
-        lst[g2][1] = lb
+        lst[g2][0] = front_sum
+        lst[g2][1] = back_sum
         finish_max(g1, ms)
         for _ in epi:
             pass
@@ -189,30 +205,23 @@
 
 
 def plan_steps(chunks, n_proj, n_out, per_chunk, send_at):
-    seq = [('P', i) for i in range(AHEAD * n_proj)]
-    p, o = AHEAD * n_proj, 0
+    half = per_chunk // 2
+    seq = [('P', i) for i in range(chunks * n_proj)] + [('F', 0)]
     for c in range(chunks):
-        seq += [('A', c * per_chunk + i) for i in range(per_chunk)]
-        if c >= chunks - SINGLE:
-            seq.append(('S', (c + 1) * per_chunk))
-        end = n_out * (c + 1 if c >= chunks - SINGLE else c)
-        seq += [('O', i) for i in range(o, end)]
-        o = end
-        if p < chunks * n_proj:
-            seq += [('P', p + i) for i in range(SPREAD)]
-            p += SPREAD
-            if p == chunks * n_proj:
-                seq.append(('F', 0))
+        seq += [('A', c * per_chunk + i) for i in range(half)]
+        if c:
+            seq += [('O', (c - 1) * n_out + i) for i in range(n_out)]
+        seq += [('A', c * per_chunk + i) for i in range(half, per_chunk)]
+    seq += [('S', chunks * per_chunk)] + [('O', (chunks - 1) * n_out + i) for i in range(n_out)]
     units = [(c * ROWS, ROWS) for c in range(chunks - SINGLE)] + [(i, 1) for i in range((chunks - SINGLE) * ROWS, chunks * ROWS)]
     first_use = [seq.index(('A', row * per_chunk // ROWS)) for row, _ in units]
-    proj, out, att, wire, inner, now = COST
+    proj, out, att, wire, pause, inner, now = COST
     took = {'P': proj, 'O': out, 'A': att, 'S': att, 'F': 0.6}
-    hops = {'own': [], 'one': [], 'two': [], 'three': [], 'in': []}
+    hops = {'one': [], 'two': [], 'three': [], 'in': []}
     link, core, got1, got2, sent = 0.0, 0.0, {}, {}, -1
     for step, (kind, i) in enumerate(seq):
         if step and seq[step - 1][0] == 'P' and seq[step - 1][1] % n_proj == send_at:
             sent = seq[step - 1][1] // n_proj
-            hops['own'].append(step)
         must = max((u for u in range(len(units)) if first_use[u] <= step + 1), default=-1)
         done = lambda name: len(hops[name])
         while done('one') < len(units) or done('two') < len(units):
@@ -221,14 +230,14 @@
                 u = done('one')
                 if units[u][0] // ROWS > sent:
                     break
-                link = max(now, link) + wire * units[u][1]
+                link = max(now, link) + wire * units[u][1] + pause
                 got1[u] = link
                 hops['one'].append(step)
             else:
                 if now < got1[u] + 3 and u > must:
                     break
                 now = max(now, got1[u])
-                link = max(now, link) + wire * units[u][1] / 2
+                link = max(now, link) + wire * units[u][1] / 2 + pause
                 core = max(now, core) + 2 * inner * units[u][1]
                 got2[u] = max(link, core)
                 hops['two'].append(step)
@@ -259,21 +268,13 @@
     total = rows * heads
     n_groups = heads // GROUP
     assert n_groups == 2
-    assert depth == w_query.shape[0] and group_cols == 2 * PAIR and n_proj % SPREAD == 0 and rows % ROWS == 0
-    assert kt == 1 and SPREAD > 2 * kt and group_cols == GROUP * HEAD_DIM and cp // CORES == 4
+    assert depth == w_query.shape[0] and group_cols == 2 * PAIR and rows % ROWS == 0
+    assert kt == 1 and n_proj > 4 and group_cols == GROUP * HEAD_DIM and cp // CORES == 4
     seq, units, hops = plan_steps(chunks, n_proj, n_out, per_chunk, 2 * kt)
     n_steps = len(seq)
-    loops = (chunks - AHEAD) * n_proj // SPREAD
-    assert 2 <= loops <= chunks - SINGLE
-    first_a = seq.index(('A', 0))
-    second_a = seq.index(('A', per_chunk))
-    flush = seq.index(('F', 0))
-    period = per_chunk + n_out + SPREAD
-    ends = [i for i in range(flush, n_steps) if i == flush or seq[i][0] != seq[i - 1][0]] + [n_steps]
-    tail = [(start, seq[start]) for start in ends[:-1]]
-    base = n_proj * AHEAD + SPREAD
-    both = n_out + SPREAD
-    last_both = base + both * (loops - 1)
+    half_chunk, period = per_chunk // 2, per_chunk + n_out
+    all_proj = n_proj * chunks
+    first_a, second_a, last_a = (seq.index(('A', 0)), seq.index(('A', per_chunk)), seq.index(('S', total)))
     n_tiles = (n_proj + n_out) * chunks
 
     def pick(cases, other):
@@ -295,40 +296,27 @@
         nxt, far, prv, mate = device(1), device(2), device(chips - 1), device(0, 1)
 
         a, r = 1 + div(s - second_a, period), rem(s - second_a, period)
-        r0 = s - first_a
-        kinds = {'A': 0, 'S': 1, 'O': 2, 'P': 3, 'F': 4}
-        parts = [
-            (s < first_a, 3, s),
-            (s < first_a + per_chunk, 0, r0),
-            (s < second_a, 3, s - per_chunk),
-            (s < flush, jnp.where(r < per_chunk, 0, jnp.where(r < per_chunk + n_out, 2, 3)),
-             jnp.where(r < per_chunk, a * per_chunk + r,
-                       jnp.where(r < per_chunk + n_out, (a - 1) * n_out + r - per_chunk, AHEAD * n_proj + a * SPREAD + r - per_chunk - n_out))),
-        ]
-        for (start, (what, i)), (stop, _) in zip(tail, tail[1:] + [(n_steps, None)]):
-            parts.append((s < stop, kinds[what], s + (i - start)))
-        kind = pick([(c, k) for c, k, _ in parts[:-1]], parts[-1][1])
-        num = pick([(c, i) for c, _, i in parts[:-1]], parts[-1][2])
-        is_new, is_skew, is_out, is_proj, is_flush = (kind == k for k in range(5))
-        is_head = kind < 2
-        n = oidx = pidx = num
+        is_proj, is_flush = s < all_proj, s == all_proj
+        in_first, is_skew = s < second_a, s == last_a
+        past = jnp.where(s > last_a, period, 0)
+        is_out = jnp.logical_or(past > 0, jnp.logical_and(jnp.logical_not(in_first), jnp.logical_and(r >= half_chunk, r < half_chunk + n_out)))
+        is_head = jnp.logical_and(s > all_proj, jnp.logical_not(is_out))
+        is_new = jnp.logical_and(is_head, jnp.logical_not(is_skew))
+        n = jnp.where(in_first, s - first_a, a * per_chunk + jnp.where(r >= half_chunk + n_out, r - n_out, r))
+        oidx = jnp.where(past > 0, s - last_a - 1 + (chunks - 1) * n_out, (a - 1) * n_out + r - half_chunk)
+        pidx = s
         oc, col = div(oidx, n_out), rem(oidx, n_out)
         pc, pt = div(pidx, n_proj), rem(pidx, n_proj)
-        tile_p = jnp.where(pidx < base, pidx, base + div(pidx - base, SPREAD) * both + n_out + rem(pidx - base, SPREAD))
-        tile_o = jnp.where(oc < loops - 1, base + oc * both + col, last_both + oidx - (loops - 1) * n_out)
+        tile_p, tile_o = pidx, all_proj + oidx
 
         def row_ds(c):
             return pl.ds(c * ROWS, ROWS)
 
         def load_tile(j):
             slot = rem(j, 2)
-            u = j - base
-            v = j - last_both
-            only_out = j >= last_both
-            is_p = jnp.logical_or(j < base, jnp.logical_and(jnp.logical_not(only_out), rem(u, both) >= n_out))
-            p = rem(jnp.where(j < base, j, base + div(u, both) * SPREAD + rem(u, both) - n_out), n_proj)
-            o_col = jnp.where(only_out, rem(v, n_out), rem(u, both))
-            o_chunk = jnp.where(only_out, loops - 1 + div(v, n_out), div(u, both))
+            is_p = j < all_proj
+            p = rem(j, n_proj)
+            o_chunk, o_col = div(j - all_proj, n_out), rem(j - all_proj, n_out)
 
             def start(w_hbm, tile_col):
                 cols = pl.ds(pl.multiple_of(tile_col * TILE, TILE), TILE)
@@ -384,35 +372,38 @@
             cols = pl.ds(pl.multiple_of(tile_col * TILE, TILE), TILE)
             return pltpu.make_async_copy(ybuf.at[slot], y_hbm.at[row_ds(c), :, cols], ysem.at[slot])
 
-        def hop(kind, row, size, part=None):
+        def hop(kind, row, size, only=None, sem=0):
             rs = pl.ds(row, size)
             src, to = {R1: (my, nxt), L1: (my, prv), X0: (my, mate), R2: (prv, nxt), L2: (nxt, prv), X1: (nxt, mate), X2: (far, mate), X3: (prv, mate)}[kind]
-            ref = kv_hbm.at[rs, src]
             if kind in (R2, L2):
-                group = 0 if kind == R2 else 1
-                ref = kv_hbm.at[rs, src, group] if part is None else kv_hbm.at[rs, src, group, part]
-            elif part is not None:
-                ref = kv_hbm.at[rs, src, part]
-            sem = 2 * row + (part or 0)
+                ref = kv_hbm.at[rs, src, 0 if kind == R2 else 1]
+            else:
+                ref = kv_hbm.at[rs, src] if only is None else kv_hbm.at[rs, src, :, only]
+            sem = 2 * row if only is None else sem
             return pltpu.make_async_remote_copy(src_ref=ref, dst_ref=ref, send_sem=send_sem.at[kind, sem], recv_sem=recv_sem.at[kind, sem],
                                                 device_id={'cp': to}, device_id_type=pl.DeviceIdType.MESH)
 
-        def ring(kinds, row, size, act):
+        def first_copies(only, act):
             @pl.when(core == 0)
             def _():
-                near(kinds, row, size, act)
-
-            @pl.when(jnp.logical_and(core != 0, size == 1))
-            def _():
-                for kind in kinds:
-                    for part in range(2):
-                        act(hop(kind, row, 1, part))
-
-            @pl.when(jnp.logical_and(core != 0, size != 1))
-            def _():
-                for kind in kinds:
+                for kind in (R1, L1):
+                    act(hop(kind, 0, ROWS, only, only))
+
+            @pl.when(core != 0)
+            def _():
+                for kind in (R1, L1):
                     for i in range(ROWS):
-                        act(hop(kind, row + i, 1))
+                        act(hop(kind, i, 1, only, ROWS * only + i))
+
+        def ring_one(row, size, act, parts=(0, 1)):
+            @pl.when(row == 0)
+            def _():
+                for only in parts:
+                    first_copies(only, act)
+
+            @pl.when(row != 0)
+            def _():
+                near((R1, L1), row, size, act)
 
         def near(kinds, row, size, act):
             @pl.when(size == 1)
@@ -428,22 +419,21 @@
         start, received, left = (lambda c: c.start()), (lambda c: c.wait_recv()), (lambda c: c.wait_send())
 
         def hop_one(row, size):
-            ring((R1, L1), row, size, start)
+            ring_one(row, size, start, (1,))
             near((X0,), row, size, start)
 
         def hop_two(row, size):
-            ring((R1, L1), row, size, received)
-            ring((R2, L2), row, size, start)
-            near((X1, X3), row, size, start)
+            ring_one(row, size, received)
+            near((R2, L2, X1, X3), row, size, start)
 
         def hop_three(row, size):
-            ring((R2, L2), row, size, received)
+            near((R2, L2), row, size, received)
             near((X2,), row, size, start)
 
         def arrive(row, size):
             near((X0, X1, X3, X2), row, size, received)
-            ring((R1, L1, R2, L2), row, size, left)
-            near((X0, X1, X3, X2), row, size, left)
+            ring_one(row, size, left)
+            near((R2, L2, X0, X1, X3, X2), row, size, left)
             for copy in load_kv(row * n_groups):
                 copy.start()
 
@@ -451,14 +441,9 @@
             def _():
                 load_q(0).start()
 
-        def own_stored(row, size):
-            first = div(row, ROWS) * n_proj
-            wait_store(first)
-            wait_store(first + 1)
-
         def unit_hops(lo, hi):
-            for name, act in (('own', own_stored), ('two', hop_two), ('one', hop_one), ('three', hop_three), ('in', arrive)):
-                due = [(step, (u * ROWS, ROWS) if name == 'own' else units[u]) for u, step in enumerate(hops[name]) if lo <= step < hi]
+            for name, act in (('two', hop_two), ('one', hop_one), ('three', hop_three), ('in', arrive)):
+                due = [(step, units[u]) for u, step in enumerate(hops[name]) if lo <= step < hi]
                 if not due:
                     continue
                 row, size = pick([(s == step, row) for step, (row, _) in due], -1), pick([(s == step, size) for step, (_, size) in due], ROWS)
@@ -515,10 +500,19 @@
         def _():
             next_tile(tile_p)
 
-            @pl.when(jnp.logical_and(pidx >= 3, jnp.logical_or(pt < 3, pt > 4)))
+            @pl.when(jnp.logical_and(pidx > 3, pt != 4))
             def _():
                 wait_store(pidx - 3)
 
+            @pl.when(pidx == 2)
+            def _():
+                wait_store(0)
+                first_copies(0, start)
+
+            @pl.when(pt == 3)
+            def _():
+                wait_store(pidx - 2)
+
             @pl.when(pt == 0)
             def _():
                 load_x(pc).wait()
@@ -527,7 +521,7 @@
             def _():
                 load_x(pc + 1).start()
 
-        spans = 4
+        spans = 6
         for i in range(spans):
             lo, hi = n_steps * i // spans, n_steps * (i + 1) // spans
 
@@ -558,12 +552,10 @@
         def _():
             g = div(n, GROUP)
 
-            @pl.when(jnp.logical_and(n < total, jnp.logical_or(is_skew, jnp.logical_or(rem(n, per_chunk) != 0, n <= total - SINGLE * per_chunk))))
+            @pl.when(is_new)
             def _():
                 load_q(n).wait()
 
-            @pl.when(is_new)
-            def _():
                 @pl.when(n + 1 < total)
                 def _():
                     load_q(n + 1).start()

time: 687 us -> 667 us (0.971)
  Pallas kernels: 658 us -> 638 us
    pallas_call x1, Pallas kernels: 658 us -> 638 us  [layer(): pl.pallas_call(kern, name='layer', grid=(n_steps,), in_specs=[any_spec, p...]
where the time goes in v1:
time: 667 us
  Pallas kernels  638 us (96%)
  local copies, waits for them, and re-layouts  23.6 us (4%)
    pallas_call x1, Pallas kernels, layer(): pl.pallas_call(kern, name='layer', grid=(n_steps,), in_specs=[any_spec, p...  638 us
    unnamed x1, local copies, waits for them, and re-layouts  22.9 us

profile of v1, /device:TPU:113, one launch (start us, length us, event | category | flops | bytes accessed | tf_op | source)
XLA Modules:
  0.0 666.8 jit_solution(3236279586606659625)
XLA Ops:
  0.0 0.1 pad_maximum_fusion
  0.1 0.7 convert_element_type.3
  0.8 0.3 broadcast_in_dim.18
  1.2 0.3 broadcast_in_dim.20
  1.5 4.9 fusion
  6.4 637.5 %layer.1 = (bf16[16,256,4096]{2,1,0:T(8,128)(2,1)}, bf16[16,8,2,2,2,4,128,128]{7,6,5,4,3,2,1,0:T(8,128)(2,1)}, bf16[16,8,2,4,128,128]{5,4,3,2,1,0:T(8,128)(2,1)}) custom-call(bf16[16,256,4096]{2,1,0:T(8,128)(2,1)} %x_hbm.1, f32[2048,128]{1,0:T(8,128)} %get-tuple-element.8.cos_ref, f32[2048,128]{1,0:T(8,128)} %get-tuple-element.7.sin_ref, ...), custom_call_target="tpu_custom_call" | custom-call | flops 498216206336 | bytes 67108864 | tf_op jit(solution)/shard_map/layer/pallas_call | solution.py:606
  643.9 22.9 %copy.8 = bf16[16,256,4096]{2,1,0:T(8,128)(2,1)} copy(bf16[16,256,4096]{2,1,0:T(8,128)(2,1)} %get-tuple-element.6) | data formatting | bytes 67108864
  (2 shorter events, 0.0 us)

commit v2 on v1

--- a/solution.py
+++ b/solution.py
@@ -16,6 +16,7 @@
 ROWS = 2
 TILE = 1024
 GROUP = 4
+STEP_HEADS = 2
 PAIR = 256
 VMEM_LIMIT = 66_000_000
 LAG = 5
@@ -23,8 +24,9 @@
 BACK = (2, 0)
 EPI = 3
 SINGLE = 2
-COST = (4.85, 4.72, 1.6, 22.8, 0.3, 1.75, 18.0)
-SPLIT = 2
+COST = (4.85, 4.72, 2.95, 22.8, 0.4, 1.75, 18.0)
+SLACK = 0.3
+SPLIT = 4
 R1, L1, X0, R2, L2, X1, X2, X3 = range(8)
 f32, bf16 = jnp.float32, jnp.bfloat16
 div, rem = lax.div, lax.rem
@@ -217,6 +219,7 @@
     first_use = [seq.index(('A', row * per_chunk // ROWS)) for row, _ in units]
     proj, out, att, wire, pause, inner, now = COST
     took = {'P': proj, 'O': out, 'A': att, 'S': att, 'F': 0.6}
+    amount = lambda u: units[u][1]
     hops = {'one': [], 'two': [], 'three': [], 'in': []}
     link, core, got1, got2, sent = 0.0, 0.0, {}, {}, -1
     for step, (kind, i) in enumerate(seq):
@@ -234,7 +237,8 @@
                 got1[u] = link
                 hops['one'].append(step)
             else:
-                if now < got1[u] + 3 and u > must:
+                slack = 3 + SLACK * wire * (amount(u + 1) if u + 1 < len(units) else 0)
+                if now < got1[u] + slack and u > must:
                     break
                 now = max(now, got1[u])
                 link = max(now, link) + wire * units[u][1] / 2 + pause
@@ -264,9 +268,8 @@
     chunks = rows // ROWS
     kt, qt, n_out = kv_cols // TILE, inner // TILE, depth // TILE
     n_proj = 2 * kt + qt
-    per_chunk = ROWS * heads
-    total = rows * heads
-    n_groups = heads // GROUP
+    per_chunk, total = ROWS * heads // STEP_HEADS, rows * heads // STEP_HEADS
+    n_groups, per_group = heads // GROUP, GROUP // STEP_HEADS
     assert n_groups == 2
     assert depth == w_query.shape[0] and group_cols == 2 * PAIR and rows % ROWS == 0
     assert kt == 1 and n_proj > 4 and group_cols == GROUP * HEAD_DIM and cp // CORES == 4
@@ -358,7 +361,8 @@
             return pltpu.make_async_copy(x_hbm.at[row_ds(c)], xbuf.at[rem(c, 2)], xsem.at[rem(c, 2)])
 
         def load_q(m):
-            return pltpu.make_async_copy(q_hbm.at[div(m, heads), rem(m, heads)], qbuf.at[rem(m, 2)], qsem.at[rem(m, 2)])
+            first = m * STEP_HEADS
+            return pltpu.make_async_copy(q_hbm.at[div(first, heads), pl.ds(rem(first, heads), STEP_HEADS)], qbuf.at[rem(m, 2)], qsem.at[rem(m, 2)])
 
         def load_kv(g):
             slot = rem(g, 2)
@@ -548,39 +552,44 @@
             wait_store(end - 2)
             wait_store(end - 1)
 
-        @pl.when(is_head)
-        def _():
-            g = div(n, GROUP)
-
-            @pl.when(is_new)
-            def _():
-                load_q(n).wait()
-
-                @pl.when(n + 1 < total)
-                def _():
-                    load_q(n + 1).start()
-
-                @pl.when(rem(n, GROUP) == 0)
-                def _():
-                    wait_kv(g)
-
-                fresh = jnp.logical_or(rem(g + 1, ROWS * n_groups) == 0, jnp.logical_and(g + 1 >= (rows - SINGLE * ROWS) * n_groups, rem(g + 1, n_groups) == 0))
-
-                @pl.when(jnp.logical_and(rem(n, GROUP) == 1, jnp.logical_not(fresh)))
-                def _():
-                    for copy in load_kv(g + 1):
-                        copy.start()
-
-            m = jnp.maximum(n - 1, 0)
-            o_slot = rem(div(m, per_chunk), 2)
-            row, head = rem(div(m, heads), ROWS), rem(m, heads)
+        def attend(head, slot, i):
+            m = jnp.maximum(head - 1, 0)
+            o_slot = rem(div(m, ROWS * heads), 2)
+            row, h = rem(div(m, heads), ROWS), rem(m, heads)
 
             def put(half, j, val):
                 rs = pl.ds(pl.multiple_of(row * tok_rows + half * half_len, half_len), half_len)
-                cs = pl.ds(pl.multiple_of(head * group_cols + j * HEAD_DIM, HEAD_DIM), HEAD_DIM)
+                cs = pl.ds(pl.multiple_of(h * group_cols + j * HEAD_DIM, HEAD_DIM), HEAD_DIM)
                 oscr[o_slot, rs, cs] = val
 
-            attn_step(n, cp, my, qbuf.at[rem(n, 2)], put, attn)
+            attn_step(head, cp, my, qbuf.at[slot, i], put, attn)
+
+        @pl.when(is_new)
+        def _():
+            g = div(n, per_group)
+            load_q(n).wait()
+
+            @pl.when(n + 1 < total)
+            def _():
+                load_q(n + 1).start()
+
+            @pl.when(rem(n, per_group) == 0)
+            def _():
+                wait_kv(g)
+
+            fresh = jnp.logical_or(rem(g + 1, ROWS * n_groups) == 0, jnp.logical_and(g + 1 >= (rows - SINGLE * ROWS) * n_groups, rem(g + 1, n_groups) == 0))
+
+            @pl.when(jnp.logical_and(rem(n, per_group) == per_group - 1, jnp.logical_not(fresh)))
+            def _():
+                for copy in load_kv(g + 1):
+                    copy.start()
+
+            for i in range(STEP_HEADS):
+                attend(n * STEP_HEADS + i, rem(n, 2), i)
+
+        @pl.when(is_skew)
+        def _():
+            attend(n * STEP_HEADS, rem(n, 2), 0)
 
         @pl.when(is_out)
         def _():
@@ -602,7 +611,7 @@
                 store_y(0, 0, y_slot).wait()
 
     any_spec = pl.BlockSpec(memory_space=pl.ANY)
-    flops = 2 * rows * tok_rows * depth * (2 * inner + 2 * kv_cols) + 8 * total * (cp + 1) * half_len * group_cols * HEAD_DIM * 2
+    flops = 2 * rows * tok_rows * depth * (2 * inner + 2 * kv_cols) + 8 * rows * heads * (cp + 1) * half_len * group_cols * HEAD_DIM * 2
     y, _, _ = pl.pallas_call(
         kern,
         name='layer',
@@ -622,7 +631,7 @@
             pltpu.VMEM((2, ROWS, fold, 2, GROUP, half_len, HEAD_DIM), bf16),
             pltpu.VMEM((2, toks, inner), bf16),
             pltpu.VMEM((2, ROWS, tok_rows, TILE), bf16),
-            pltpu.VMEM((2, 2, group_cols // HEAD_DIM, half_len, HEAD_DIM), bf16),
+            pltpu.VMEM((2, STEP_HEADS, 2, group_cols // HEAD_DIM, half_len, HEAD_DIM), bf16),
             pltpu.SemaphoreType.DMA((2,)),
             pltpu.SemaphoreType.DMA((2,)),
             pltpu.SemaphoreType.DMA((2,)),

time: 667 us -> 650 us (0.975)
  Pallas kernels: 638 us -> 621 us
    pallas_call x1, Pallas kernels: 638 us -> 621 us  [layer(): pl.pallas_call(kern, name='layer', grid=(n_steps,), in_specs=[any_spec, p...]
where the time goes in v2:
time: 650 us
  Pallas kernels  621 us (96%)
  local copies, waits for them, and re-layouts  23.6 us (4%)
    pallas_call x1, Pallas kernels, layer(): pl.pallas_call(kern, name='layer', grid=(n_steps,), in_specs=[any_spec, p...  621 us
    unnamed x1, local copies, waits for them, and re-layouts  22.9 us

profile of v2, /device:TPU:113, one launch (start us, length us, event | category | flops | bytes accessed | tf_op | source)
XLA Modules:
  0.0 649.8 jit_solution(7446766280966920440)
XLA Ops:
  0.0 0.1 pad_maximum_fusion
  0.1 0.7 convert_element_type.3
  0.8 0.3 broadcast_in_dim.18
  1.2 0.3 broadcast_in_dim.20
  1.5 4.9 fusion
  6.4 620.6 %layer.1 = (bf16[16,256,4096]{2,1,0:T(8,128)(2,1)}, bf16[16,8,2,2,2,4,128,128]{7,6,5,4,3,2,1,0:T(8,128)(2,1)}, bf16[16,8,2,4,128,128]{5,4,3,2,1,0:T(8,128)(2,1)}) custom-call(bf16[16,256,4096]{2,1,0:T(8,128)(2,1)} %x_hbm.1, f32[2048,128]{1,0:T(8,128)} %get-tuple-element.8.cos_ref, f32[2048,128]{1,0:T(8,128)} %get-tuple-element.7.sin_ref, ...), custom_call_target="tpu_custom_call" | custom-call | flops 498216206336 | bytes 67108864 | tf_op jit(solution)/shard_map/layer/pallas_call | solution.py:615
  626.9 22.9 %copy.8 = bf16[16,256,4096]{2,1,0:T(8,128)(2,1)} copy(bf16[16,256,4096]{2,1,0:T(8,128)(2,1)} %get-tuple-element.6) | data formatting | bytes 67108864
  (2 shorter events, 0.0 us)

commit v3 on v2

--- a/solution.py
+++ b/solution.py
@@ -16,7 +16,7 @@
 ROWS = 2
 TILE = 1024
 GROUP = 4
-STEP_HEADS = 2
+STEP_HEADS = 4
 PAIR = 256
 VMEM_LIMIT = 66_000_000
 LAG = 5
@@ -24,7 +24,7 @@
 BACK = (2, 0)
 EPI = 3
 SINGLE = 2
-COST = (4.85, 4.72, 2.95, 22.8, 0.4, 1.75, 18.0)
+COST = (4.85, 4.72, 4.9, 22.8, 0.4, 1.75, 18.0)
 SLACK = 0.3
 SPLIT = 4
 R1, L1, X0, R2, L2, X1, X2, X3 = range(8)
@@ -53,7 +53,8 @@
     blocks = sum(1 if isinstance(t, str) else 2 for t in steps)
     groups = lambda *shape: [pltpu.VMEM(shape, f32), pltpu.VMEM(shape, f32)]
     return [
-        pltpu.VMEM((2, cp, 2, 2, GROUP, HEAD_DIM, half_len), bf16),
+        pltpu.VMEM((2, cp, 2, GROUP, half_len, HEAD_DIM), bf16),
+        pltpu.VMEM((3, cp, 2, GROUP, HEAD_DIM, half_len), bf16),
         *groups(blocks * half_len, PAIR),
         *groups(1 + len(BACK), HEAD_DIM, PAIR),
         *groups(cp // 2 + 1, HEAD_DIM, PAIR),
@@ -64,7 +65,7 @@
 
 
 def attn_init(cp, scratch):
-    _, _, _, _, _, pv0, pv1, _, _, _, _, bias = scratch
+    _, _, _, _, _, _, pv0, pv1, _, _, _, _, bias = scratch
     kpos = lax.broadcasted_iota(jnp.int32, bias.shape, 0)
     qpos = lax.broadcasted_iota(jnp.int32, bias.shape, 1)
     for ref in (pv0, pv1):
@@ -73,13 +74,13 @@
 
 
 def attn_step(n, cp, my, q_ref, put, scratch):
-    kvbuf, sc0, sc1, ac0, ac1, pv0, pv1, mx0, mx1, sm0, sm1, bias = scratch
+    kbuf, vbuf, sc0, sc1, ac0, ac1, pv0, pv1, mx0, mx1, sm0, sm1, bias = scratch
     sbuf, acc, pvb, mst, lst = (sc0, sc1), (ac0, ac1), (pv0, pv1), (mx0, mx1), (sm0, sm1)
     steps, parts = attn_steps(cp), cp // 2
-    half_len = kvbuf.shape[6]
-    here = (rem(div(n, GROUP), 2), rem(n, GROUP))
+    half_len = kbuf.shape[4]
+    here, k_slot = (rem(div(n, GROUP), 3), rem(n, GROUP)), rem(div(n, GROUP), 2)
     before = jnp.maximum(n - 1, 0)
-    behind_ = (rem(div(before, GROUP), 2), rem(before, GROUP))
+    behind_ = (rem(div(before, GROUP), 3), rem(before, GROUP))
     pairs, par = div(my, 2), rem(my, 2)
 
     def place(j):
@@ -115,8 +116,8 @@
         return items[0] if len(items) == 1 else jnp.concatenate(items, axis=axis)
 
     def scores(t, g):
-        slot, e = here
-        k = stack([kvbuf[slot, s, 0, f, e] for s, f in locs[t]], 0)
+        e = here[1]
+        k = stack([kbuf[k_slot, s, f, e] for s, f in locs[t]], 0)
         s = lax.dot_general(k, q_ref[half_of(t), 2 * g:2 * g + 2].reshape(PAIR, HEAD_DIM), (((1,), (1,)), ((), ())), preferred_element_type=f32)
         if t in ('front', 'back'):
             b = bias[...]
@@ -146,7 +147,7 @@
 
     def put_weighted(g, ts, ps, at):
         slot, e = at
-        vals = stack([kvbuf[slot, s, 1, f, e] for t in ts for s, f in locs[t]], 1)
+        vals = stack([vbuf[slot, s, f, e] for t in ts for s, f in locs[t]], 1)
         out = lax.dot_general(vals, stack(ps, 0), (((1,), (0,)), ((), ())), preferred_element_type=f32)
         if ts[0] in part_of:
             pvb[g][part_of[ts[0]]] = out
@@ -285,9 +286,9 @@
             other = jnp.where(cond, val, other)
         return other
 
-    def kern(x_hbm, cos_ref, sin_ref, wq_hbm, wk_hbm, wv_hbm, wo_hbm, y_hbm, kv_hbm, q_hbm,
-             wbuf, xbuf, xres, raw, stage, oscr, ybuf, qbuf,
-             wsem, xsem, rsem, osem, ysem, qsem, kvsem, send_sem, recv_sem, *attn):
+    def kern(x_hbm, cos_hbm, sin_hbm, wq_hbm, wk_hbm, wv_hbm, wo_hbm, y_hbm, kv_hbm, q_hbm,
+             wbuf, xbuf, tables, xres, raw, stage, oscr, ybuf, qbuf,
+             wsem, xsem, tsem, rsem, osem, ysem, qsem, ksem, vsem, send_sem, recv_sem, *attn):
         s = pl.program_id(0)
         my = lax.axis_index('cp')
         chip, core = div(my, CORES), rem(my, CORES)
@@ -360,17 +361,22 @@
         def load_x(c):
             return pltpu.make_async_copy(x_hbm.at[row_ds(c)], xbuf.at[rem(c, 2)], xsem.at[rem(c, 2)])
 
+        def load_tables(c):
+            ts, slot = pl.ds(pl.multiple_of(c * ROWS * half_len, ROWS * half_len), ROWS * half_len), rem(c, 2)
+            return [pltpu.make_async_copy(src.at[ts], tables.at[slot, i], tsem.at[slot]) for i, src in enumerate((cos_hbm, sin_hbm))]
+
         def load_q(m):
             first = m * STEP_HEADS
             return pltpu.make_async_copy(q_hbm.at[div(first, heads), pl.ds(rem(first, heads), STEP_HEADS)], qbuf.at[rem(m, 2)], qsem.at[rem(m, 2)])
 
         def load_kv(g):
-            slot = rem(g, 2)
-            return [pltpu.make_async_copy(kv_hbm.at[div(g, n_groups), src, rem(g, n_groups)], attn[0].at[slot, src], kvsem.at[slot]) for src in range(cp)]
+            row, group, slots = div(g, n_groups), rem(g, n_groups), (rem(g, 2), rem(g, 3))
+            return [pltpu.make_async_copy(kv_hbm.at[row, src, group, i], attn[i].at[slots[i], src], sem.at[slots[i]])
+                    for i, sem in enumerate((ksem, vsem)) for src in range(cp)]
 
         def wait_kv(g):
-            slot = rem(g, 2)
-            pltpu.make_async_copy(kv_hbm.at[0, :, 0], attn[0].at[slot], kvsem.at[slot]).wait()
+            for i, (sem, slot) in enumerate(((ksem, rem(g, 2)), (vsem, rem(g, 3)))):
+                pltpu.make_async_copy(kv_hbm.at[0, :, 0, i], attn[i].at[slot], sem.at[slot]).wait()
 
         def store_y(c, tile_col, slot):
             cols = pl.ds(pl.multiple_of(tile_col * TILE, TILE), TILE)
@@ -462,6 +468,8 @@
             for to in (nxt, prv, mate):
                 pl.semaphore_signal(barrier, inc=1, device_id={'cp': to}, device_id_type=pl.DeviceIdType.MESH)
             load_x(0).start()
+            for copy in load_tables(0):
+                copy.start()
             load_tile(0)
             attn_init(cp, attn)
             pl.semaphore_wait(barrier, 3)
@@ -487,8 +495,8 @@
             is_v = rem(p, n_proj) == 1
             low_lanes = lax.broadcasted_iota(jnp.int32, (half_len, HEAD_DIM), 1) < HEAD_DIM // 2
             for i in range(ROWS):
-                ts = pl.ds(pl.multiple_of((c * ROWS + i) * half_len, half_len), half_len)
-                cos, sin = cos_ref[ts], sin_ref[ts]
+                ts = slice(i * half_len, (i + 1) * half_len)
+                cos, sin = tables[rem(c, 2), 0, ts], tables[rem(c, 2), 1, ts]
                 cos_r, sin_r = pltpu.roll(cos, HEAD_DIM // 2, 1), pltpu.roll(sin, HEAD_DIM // 2, 1)
                 for half in range(2):
                     cos_h = jnp.where(low_lanes, cos, cos_r) if half == 0 else jnp.where(low_lanes, cos_r, cos)
@@ -521,9 +529,18 @@
             def _():
                 load_x(pc).wait()
 
-            @pl.when(jnp.logical_and(pt == 1, pc + 1 < chunks))
-            def _():
-                load_x(pc + 1).start()
+            @pl.when(jnp.where(pc == 0, pt == 0, pt == 1))
+            def _():
+                for copy in load_tables(pc):
+                    copy.wait()
+
+            @pl.when(pt == 1)
+            def _():
+                @pl.when(pc + 1 < chunks)
+                def _():
+                    load_x(pc + 1).start()
+                    for copy in load_tables(pc + 1):
+                        copy.start()
 
         spans = 6
         for i in range(spans):
@@ -579,7 +596,7 @@
 
             fresh = jnp.logical_or(rem(g + 1, ROWS * n_groups) == 0, jnp.logical_and(g + 1 >= (rows - SINGLE * ROWS) * n_groups, rem(g + 1, n_groups) == 0))
 
-            @pl.when(jnp.logical_and(rem(n, per_group) == per_group - 1, jnp.logical_not(fresh)))
+            @pl.when(jnp.logical_and(rem(n, per_group) == 0, jnp.logical_not(fresh)))
             def _():
                 for copy in load_kv(g + 1):
                     copy.start()
@@ -616,7 +633,7 @@
         kern,
         name='layer',
         grid=(n_steps,),
-        in_specs=[any_spec, pl.BlockSpec(memory_space=pltpu.VMEM), pl.BlockSpec(memory_space=pltpu.VMEM)] + [any_spec] * 4,
+        in_specs=[any_spec] * 7,
         out_specs=[any_spec] * 3,
         out_shape=[
             jax.ShapeDtypeStruct(x_loc.shape, bf16),
@@ -626,6 +643,7 @@
         scratch_shapes=[
             pltpu.VMEM((2, depth, TILE), bf16),
             pltpu.VMEM((2, ROWS, tok_rows, depth), bf16),
+            pltpu.VMEM((2, 2, ROWS * half_len, HEAD_DIM), f32),
             pltpu.VMEM((2, ROWS, tok_rows, TILE), bf16),
             pltpu.VMEM((toks, TILE), bf16),
             pltpu.VMEM((2, ROWS, fold, 2, GROUP, half_len, HEAD_DIM), bf16),
@@ -639,6 +657,8 @@
             pltpu.SemaphoreType.DMA((2,)),
             pltpu.SemaphoreType.DMA((2,)),
             pltpu.SemaphoreType.DMA((2,)),
+            pltpu.SemaphoreType.DMA((2,)),
+            pltpu.SemaphoreType.DMA((3,)),
             pltpu.SemaphoreType.DMA((8, 2 * rows)),
             pltpu.SemaphoreType.DMA((8, 2 * rows)),
         ] + attn_scratch(cp, half_len),

time: 650 us -> 649 us (level)
  no operation moved by 1% of the time
where the time goes in v3:
time: 649 us
  Pallas kernels  620 us (96%)
  local copies, waits for them, and re-layouts  23.6 us (4%)
    pallas_call x1, Pallas kernels, layer(): pl.pallas_call(kern, name='layer', grid=(n_steps,), in_specs=[any_spec] *...  620 us
    unnamed x1, local copies, waits for them, and re-layouts  22.9 us

profile of v3, /device:TPU:113, one launch (start us, length us, event | category | flops | bytes accessed | tf_op | source)
XLA Modules:
  0.0 649.2 jit_solution(5849171625893530452)
XLA Ops:
  0.0 0.1 pad_maximum_fusion
  0.1 0.7 convert_element_type.3
  0.8 0.3 broadcast_in_dim.18
  1.2 0.3 broadcast_in_dim.20
  1.5 4.9 fusion
  6.4 620.0 %layer.1 = (bf16[16,256,4096]{2,1,0:T(8,128)(2,1)}, bf16[16,8,2,2,2,4,128,128]{7,6,5,4,3,2,1,0:T(8,128)(2,1)}, bf16[16,8,2,4,128,128]{5,4,3,2,1,0:T(8,128)(2,1)}) custom-call(bf16[16,256,4096]{2,1,0:T(8,128)(2,1)} %x_hbm.1, f32[2048,128]{1,0:T(8,128)} %get-tuple-element.8.cos_hbm, f32[2048,128]{1,0:T(8,128)} %get-tuple-element.7.sin_hbm, ...), custom_call_target="tpu_custom_call" | custom-call | flops 498216206336 | bytes 67108864 | tf_op jit(solution)/shard_map/layer/pallas_call | solution.py:632
  626.3 22.9 %copy.8 = bf16[16,256,4096]{2,1,0:T(8,128)(2,1)} copy(bf16[16,256,4096]{2,1,0:T(8,128)(2,1)} %get-tuple-element.6) | data formatting | bytes 67108864
  (2 shorter events, 0.0 us)
